TPU v7x, 32 devices: a whole 2x2x4 slice. The times are simulated.
32 devices in a mesh: bank: 4 (over z), zero: 8 (over y, x, core).
Axes of the slice: x: 2, y: 2, z: 4, core: 2. Of those that a mesh axis runs over, the one named last changes fastest.
Arguments:
- master_gate: float32 [64, 2048, 1024], P('bank', 'zero'), may hold values from -0.1875 to 0.1875
- second_gate: bfloat16 [64, 2048, 1024], P('bank', 'zero'), may hold values from -0.0625 to 0.0625
- master_up: float32 [64, 2048, 1024], P('bank', 'zero'), may hold values from -0.1875 to 0.1875
- second_up: bfloat16 [64, 2048, 1024], P('bank', 'zero'), may hold values from -0.0625 to 0.0625
- master_down: float32 [64, 1024, 2048], P('bank', None, 'zero'), may hold values from -0.25 to 0.25
- second_down: bfloat16 [64, 1024, 2048], P('bank', None, 'zero'), may hold values from -0.09375 to 0.09375
- router_weight: float32 [2048, 64], P('zero', 'bank'), may hold values from -0.125 to 0.125
- router_gain: float32 [2048], P('zero'), may hold values from 0.25 to 1.75
Outputs:
- final_gate: bfloat16 [64, 2048, 1024], P('bank', None, 'zero')
- final_up: bfloat16 [64, 2048, 1024], P('bank', None, 'zero')
- final_down: bfloat16 [64, 1024, 2048], P('bank', 'zero')
- scale_gate: float32 [64, 1024], P('bank', 'zero')
- scale_up: float32 [64, 1024], P('bank', 'zero')
- scale_down: float32 [64, 1024], P('bank', 'zero')
- serve_router: bfloat16 [2048, 64], replicated
All inputs are finite; a program needn't handle non-finite values. Where the computation divides by a largest or mean magnitude, that divisor is 1e-20 or more.
Results may differ from a plain program's by a relative error of at most 0.001.
Values may be sent and summed in bfloat16 or wider, within the bound.
A program may use at most 192 MiB of HBM per device.

v0:
```python
import jax
import jax.numpy as jnp
from jax import lax
from jax.sharding import PartitionSpec as P

D_MODEL = 2048


def on_device(
    master_gate,
    second_gate,
    master_up,
    second_up,
    master_down,
    second_down,
    router_weight,
    router_gain,
):
    merged_gate = master_gate + second_gate.astype(jnp.float32)
    merged_up = master_up + second_up.astype(jnp.float32)
    merged_down = master_down + second_down.astype(jnp.float32)
    total_gate, total_up, total_down = lax.psum(
        (
            jnp.sum(jnp.abs(merged_gate), axis=1),
            jnp.sum(jnp.abs(merged_up), axis=1),
            jnp.sum(jnp.abs(merged_down), axis=2),
        ),
        "zero",
    )
    scale_gate = total_gate / D_MODEL
    scale_up = total_up / D_MODEL
    scale_down = total_down / D_MODEL
    narrow_gate, narrow_up, narrow_down = (
        (merged_gate / jnp.expand_dims(scale_gate, 1)).astype(jnp.bfloat16),
        (merged_up / jnp.expand_dims(scale_up, 1)).astype(jnp.bfloat16),
        (merged_down / jnp.expand_dims(scale_down, 2)).astype(jnp.bfloat16),
    )
    final_gate, final_up = (
        lax.all_to_all(narrow_gate, "zero", split_axis=2, concat_axis=1, tiled=True),
        lax.all_to_all(narrow_up, "zero", split_axis=2, concat_axis=1, tiled=True),
    )
    final_down = lax.all_to_all(narrow_down, "zero", split_axis=1, concat_axis=2, tiled=True)
    scale_gate = lax.dynamic_slice_in_dim(
        scale_gate, lax.axis_index("zero") * final_gate.shape[2], final_gate.shape[2], axis=1
    )
    scale_up = lax.dynamic_slice_in_dim(
        scale_up, lax.axis_index("zero") * final_up.shape[2], final_up.shape[2], axis=1
    )
    scale_down = lax.dynamic_slice_in_dim(
        scale_down, lax.axis_index("zero") * final_down.shape[1], final_down.shape[1], axis=1
    )
    part_router = (router_weight * router_gain[:, None]).astype(jnp.bfloat16)
    row_router = lax.all_gather(part_router, "zero", axis=0, tiled=True)
    serve_router = lax.all_gather(row_router, "bank", axis=1, tiled=True)
    return (final_gate, final_up, final_down, scale_gate, scale_up, scale_down, serve_router)


def solution(mesh):
    return jax.shard_map(
        on_device,
        mesh=mesh,
        in_specs=(
            P("bank", "zero", None),
            P("bank", "zero", None),
            P("bank", "zero", None),
            P("bank", "zero", None),
            P("bank", None, "zero"),
            P("bank", None, "zero"),
            P("zero", "bank"),
            P("zero"),
        ),
        out_specs=(
            P("bank", None, "zero"),
            P("bank", None, "zero"),
            P("bank", "zero", None),
            P("bank", "zero"),
            P("bank", "zero"),
            P("bank", "zero"),
            P(),
        ),
        check_vma=False,
    )
```

profile of v0, /device:TPU:0, one launch (start us, length us, event | category | flops | bytes accessed | tf_op | source)
XLA Modules:
  0.0 554.7 jit_solution(10408405090956699153)
XLA Ops:
  7.2 17.6 %copy.31 = f32[16,256,1024]{1,0,2:T(8,128)} copy(f32[16,256,1024]{2,1,0:T(8,128)} %param.8) | data formatting | bytes 33554432 | tf_op args[0]
  24.8 17.6 %copy.34 = f32[16,256,1024]{1,0,2:T(8,128)} copy(f32[16,256,1024]{2,1,0:T(8,128)} %param.10) | data formatting | bytes 33554432 | tf_op args[2]
  42.4 12.5 %copy.30 = bf16[16,256,1024]{1,0,2:T(8,128)(2,1)} copy(bf16[16,256,1024]{2,1,0:T(8,128)(2,1)} %param.9) | data formatting | bytes 16777216 | tf_op args[1]
  54.9 12.5 %copy.33 = bf16[16,256,1024]{1,0,2:T(8,128)(2,1)} copy(bf16[16,256,1024]{2,1,0:T(8,128)(2,1)} %param.11) | data formatting | bytes 16777216 | tf_op args[3]
  67.4 25.3 %abs_reduce_fusion = f32[16,1024]{0,1:T(8,128)} fusion(f32[16,1024,256]{2,1,0:T(8,128)} %param.12, bf16[16,1024,256]{2,1,0:T(8,128)(2,1)} %param.13), kind=kLoop, calls=%fused_computation.2 | loop fusion | flops 16760832 | bytes 25231360 | tf_op jit(solution)/shard_map/reduce_sum | solution.py:26
  92.7 13.2 %abs_reduce_fusion.1 = (f32[16,1024]{0,1:T(8,128)}, f32[16,1024]{0,1:T(8,128)}) fusion(f32[16,256,1024]{1,0,2:T(8,128)} %copy.34, bf16[16,256,1024]{1,0,2:T(8,128)(2,1)S(1)} %copy-done.1, f32[16,256,1024]{1,0,2:T(8,128)} %copy.31, bf16[16,256,1024]{1,0,2:T(8,128)(2,1)S(1)} %copy-done), kind=kLoop, calls=%fused_computation.4 | loop fusion | flops 33521664 | bytes 50462720 | tf_op jit(solution)/shard_map/reduce_sum | solution.py:25
  105.9 62.0 %all-reduce.3.cloned.1.call-done = (f32[16,1024]{0,1:T(8,128)}, f32[16,1024]{0,1:T(8,128)}, f32[16,1024]{0,1:T(8,128)}) async-done(((f32[16,1024]{0,1:T(8,128)}, f32[16,1024]{0,1:T(8,128)}, f32[16,1024]{0,1:T(8,128)}), (f32[16,1024]{0,1:T(8,128)}, f32[16,1024]{0,1:T(8,128)}, f32[16,1024]{0,1:T(8,128)})) %all-reduce.3.cloned.1.call-update) | async-done | bytes 196624 | tf_op jit(solution)/shard_map/psum | solution.py:22
  167.9 1.1 broadcast_multiply_fusion.1
  169.0 12.0 %divide_convert_fusion.1 = bf16[16,256,1024]{1,0,2:T(8,128)(2,1)} fusion(f32[16,256,1024]{1,0,2:T(8,128)} %copy.34, bf16[16,256,1024]{1,0,2:T(8,128)(2,1)} %copy.33, f32[16,1024]{0,1:T(8,128)S(1)} %broadcast_multiply_fusion.1), kind=kLoop, calls=%fused_computation.3 | loop fusion | flops 16777216 | bytes 33619968 | tf_op jit(solution)/shard_map/convert_element_type | solution.py:35
  180.9 5.1 all-to-all-start.1
  186.1 12.0 %divide_convert_fusion.2 = bf16[16,256,1024]{1,0,2:T(8,128)(2,1)} fusion(f32[16,256,1024]{1,0,2:T(8,128)} %copy.31, bf16[16,256,1024]{1,0,2:T(8,128)(2,1)} %copy.30, f32[16,1024]{0,1:T(8,128)S(1)} %broadcast_multiply_fusion.2), kind=kLoop, calls=%fused_computation.6 | loop fusion | flops 16777216 | bytes 33619968 | tf_op jit(solution)/shard_map/convert_element_type | solution.py:34
  198.1 82.0 %all-to-all-done.1 = bf16[16,256,1024]{1,0,2:T(8,128)(2,1)} async-done(((bf16[16,256,1024]{1,0,2:T(8,128)(2,1)}), bf16[16,256,1024]{1,0,2:T(8,128)(2,1)}, u32[]{:S(2)}, u32[]{:S(2)}) %all-to-all-start.1) | async-done | bytes 8388640 | tf_op jit(solution)/shard_map/all_to_all | solution.py:40
  280.1 5.1 all-to-all-start
  285.3 23.8 %divide_convert_fusion = bf16[16,1024,256]{2,0,1:T(8,128)(2,1)} fusion(f32[16,1024,256]{2,1,0:T(8,128)} %param.12, f32[16,1024]{0,1:T(8,128)S(1)} %broadcast_multiply_fusion, bf16[16,1024,256]{2,1,0:T(8,128)(2,1)} %param.13), kind=kLoop, calls=%fused_computation.1 | loop fusion | flops 16777216 | bytes 33619968 | tf_op jit(solution)/shard_map/convert_element_type | solution.py:36
  309.0 70.0 %all-to-all-done = bf16[16,256,1024]{1,0,2:T(8,128)(2,1)} async-done(((bf16[16,256,1024]{1,0,2:T(8,128)(2,1)}), bf16[16,256,1024]{1,0,2:T(8,128)(2,1)}, u32[]{:S(2)}, u32[]{:S(2)}) %all-to-all-start) | async-done | bytes 8388640 | tf_op jit(solution)/shard_map/all_to_all | solution.py:39
  379.1 5.0 all-to-all-start.2
  384.1 97.2 %all_gather.6 = bf16[2048,16]{0,1:T(8,128)(2,1)S(1)} all-gather(bf16[256,16]{0,1:T(8,128)(2,1)S(1)} %multiply_convert_fusion), channel_id=1, replica_groups=mesh['bank'=4,'zero'=8] {'zero'}, dimensions={0}, use_global_device_ids=true | all-gather | bytes 73728 | tf_op jit(solution)/shard_map/all_gather | solution.py:53
  481.3 14.4 %all_gather.7 = bf16[2048,64]{0,1:T(8,128)(2,1)S(1)} all-gather(bf16[2048,16]{0,1:T(8,128)(2,1)S(1)} %all_gather.6), channel_id=1, replica_groups=mesh['bank'=4,'zero'=8] {'bank'}, dimensions={1}, use_global_device_ids=true | all-gather | bytes 327680 | tf_op jit(solution)/shard_map/all_gather | solution.py:54
  495.7 0.7 copy.39
  497.8 12.3 %copy.35 = bf16[16,8,256,128]{3,2,1,0:T(8,128)(2,1)} copy(bf16[16,8,256,128]{2,0,3,1:T(8,128)(2,1)} %bitcast.4) | data formatting | bytes 16777216 | tf_op jit(solution)/shard_map/all_to_all | solution.py:40
  510.0 12.3 %copy.32 = bf16[16,8,256,128]{3,2,1,0:T(8,128)(2,1)} copy(bf16[16,8,256,128]{2,0,3,1:T(8,128)(2,1)} %bitcast.1) | data formatting | bytes 16777216 | tf_op jit(solution)/shard_map/all_to_all | solution.py:39
  522.3 11.4 %copy.38 = bf16[16,128,8,256]{3,2,1,0:T(8,128)(2,1)} copy(bf16[16,128,8,256]{3,0,1,2:T(8,128)(2,1)} %bitcast.7) | data formatting | bytes 16777216 | tf_op jit(solution)/shard_map/all_to_all | solution.py:42
  533.7 13.4 %all_to_all.50 = bf16[16,128,2048]{2,1,0:T(8,128)(2,1)} reshape(bf16[16,128,8,256]{3,2,1,0:T(8,128)(2,1)} %copy.38) | data formatting | bytes 16777216 | tf_op jit(solution)/shard_map/all_to_all | solution.py:42
  547.1 0.7 copy.53
  (23 shorter events, 1.5 us)
Async XLA Ops:
  7.2 160.7 %all-reduce.3.cloned.1.call-start = ((), (), s32[]{:S(2)}) async-start(), calls=%async_computation.3 | async-start | bytes 3145728 | tf_op jit(solution)/shard_map/psum | solution.py:22
  67.4 25.3 %copy-start = (bf16[16,256,1024]{1,0,2:T(8,128)(2,1)S(1)}, bf16[16,256,1024]{1,0,2:T(8,128)(2,1)}, u32[]{:S(2)}) copy-start(bf16[16,256,1024]{1,0,2:T(8,128)(2,1)} %copy.30) | copy-start | bytes 25165828
  67.4 25.3 %copy-start.1 = (bf16[16,256,1024]{1,0,2:T(8,128)(2,1)S(1)}, bf16[16,256,1024]{1,0,2:T(8,128)(2,1)}, u32[]{:S(2)}) copy-start(bf16[16,256,1024]{1,0,2:T(8,128)(2,1)} %copy.33) | copy-start | bytes 25165828
  180.9 5.1 copy-start.3
  180.9 99.1 %all-to-all-start.1 = ((bf16[16,256,1024]{1,0,2:T(8,128)(2,1)}), bf16[16,256,1024]{1,0,2:T(8,128)(2,1)}, u32[]{:S(2)}, u32[]{:S(2)}) async-start(bf16[16,256,1024]{1,0,2:T(8,128)(2,1)} %divide_convert_fusion.1), calls=%async_computation.1 | async-start | bytes 16777216 | tf_op jit(solution)/shard_map/all_to_all | solution.py:40
  198.1 87.1 %copy-start.2 = (f32[16,1024]{0,1:T(8,128)S(1)}, f32[16,1024]{0,1:T(8,128)}, u32[]{:S(2)}) copy-start(f32[16,1024]{0,1:T(8,128)} %get-tuple-element.16) | copy-start | bytes 196612
  280.1 99.0 %all-to-all-start = ((bf16[16,256,1024]{1,0,2:T(8,128)(2,1)}), bf16[16,256,1024]{1,0,2:T(8,128)(2,1)}, u32[]{:S(2)}, u32[]{:S(2)}) async-start(bf16[16,256,1024]{1,0,2:T(8,128)(2,1)} %divide_convert_fusion.2), calls=%async_computation | async-start | bytes 16777216 | tf_op jit(solution)/shard_map/all_to_all | solution.py:39
  309.0 75.1 %copy-start.4 = (f32[256,16]{0,1:T(8,128)S(1)}, f32[256,16]{0,1:T(8,128)}, u32[]{:S(2)}) copy-start(f32[256,16]{0,1:T(8,128)} %param.14) | copy-start | bytes 49156
  309.0 75.1 %copy-start.5 = (f32[256]{0:T(256)S(1)}, f32[256]{0:T(256)}, u32[]{:S(2)}) copy-start(f32[256]{0:T(256)} %param.15) | copy-start | bytes 3076
  379.1 143.3 %all-to-all-start.2 = ((bf16[16,1024,256]{2,0,1:T(8,128)(2,1)}), bf16[16,1024,256]{2,0,1:T(8,128)(2,1)}, u32[]{:S(2)}, u32[]{:S(2)}) async-start(bf16[16,1024,256]{2,0,1:T(8,128)(2,1)} %divide_convert_fusion), calls=%async_computation.2 | async-start | bytes 16777216 | tf_op jit(solution)/shard_map/all_to_all | solution.py:42
Sparse Core Ops, SparseCore 0:
  106.0 61.7 all-reduce.2
where the time goes:
time: 557 us; the launch traced here: 555 us
  waiting for transfers between devices  214 us (38%)
  local copies, waits for them, and re-layouts  112 us (20%)
  blocking collectives  112 us (20%)
  other arithmetic  87.4 us (16%)
  starting transfers between devices  15.3 us (3%)
  between operations  14.1 us (3%)
    all_gather x1, blocking collectives, on_device(): row_router = lax.all_gather(part_router, 'zero', axis=0, tiled=True)  97.2 us
    all_to_all x1, waiting for transfers between devices, on_device(): lax.all_to_all(narrow_up, 'zero', split_axis=2, concat_axis=1, tiled=True)  82 us
    all_to_all x1, waiting for transfers between devices, on_device(): lax.all_to_all(narrow_gate, 'zero', split_axis=2, concat_axis=1, tiled=True)  70 us
    unnamed x20, local copies, waits for them, and re-layouts  62.9 us
    psum x1, waiting for transfers between devices, on_device(): lax.psum((jnp.sum(jnp.abs(merged_gate), axis=1), jnp.sum(jnp.abs(merged_u...  62 us
    reduce_sum x1, other arithmetic, on_device(): jnp.sum(jnp.abs(merged_down), axis=2)  25.3 us
    all_to_all x2, local copies, waits for them, and re-layouts, on_device(): lax.all_to_all(narrow_down, 'zero', split_axis=1, concat_axis=2, tiled=True)  24.8 us
    convert_element_type x1, other arithmetic, on_device(): (merged_down / jnp.expand_dims(scale_down, 2)).astype(jnp.bfloat16)  23.8 us
  transfers between devices with their start and end apart: 4, of which 3 were waited for; matrix products, arithmetic and copies ran while one was open for 11% of the time, Pallas kernels for 0%

commit v1 on v0

v1 whole, which is shorter than its diff:
```python
import jax
import jax.numpy as jnp
from jax import lax
from jax.experimental import pallas as pl
from jax.experimental.pallas import tpu as pltpu
from jax.sharding import PartitionSpec as P

f32, bf16 = jnp.float32, jnp.bfloat16


def cost(read_write, flops):
    return pl.CostEstimate(flops=flops, bytes_accessed=read_write, transcendentals=0)


def to_all(part, axes, count):
    same = jnp.broadcast_to(part[None], (count,) + part.shape)
    return lax.all_to_all(same, axes, split_axis=0, concat_axis=0, tiled=True)


def narrow_columns(master, second, inverse, zero):
    experts, rows, width = master.shape
    piece = width // zero
    step = 2 if experts % 2 == 0 else 1

    def body(master_ref, second_ref, inverse_ref, out_ref):
        for k in range(zero):
            cut = slice(k * piece, (k + 1) * piece)
            merged = master_ref[:, :, cut] + second_ref[:, :, cut].astype(f32)
            out_ref[k] = (merged * inverse_ref[:, :, cut]).astype(bf16)

    block = pl.BlockSpec((step, rows, width), lambda i: (i, 0, 0))
    return pl.pallas_call(
        body,
        grid=(experts // step,),
        in_specs=[block, block, pl.BlockSpec((step, 1, width), lambda i: (i, 0, 0))],
        out_specs=pl.BlockSpec((zero, step, rows, piece), lambda i: (0, i, 0, 0)),
        out_shape=jax.ShapeDtypeStruct((zero, experts, rows, piece), bf16),
        cost_estimate=cost(8 * master.size, 2 * master.size),
    )(master, second, inverse)


def join(pieces, axis):
    zero, experts, rows, columns = pieces.shape
    step = 2 if experts % 2 == 0 else 1
    shape = (zero * rows, columns) if axis == 1 else (rows, zero * columns)

    def body(in_ref, out_ref):
        for k in range(zero):
            if axis == 1:
                out_ref[:, k * rows : (k + 1) * rows, :] = in_ref[k]
            else:
                out_ref[:, :, k * columns : (k + 1) * columns] = in_ref[k]

    return pl.pallas_call(
        body,
        grid=(experts // step,),
        in_specs=[pl.BlockSpec((zero, step, rows, columns), lambda i: (0, i, 0, 0))],
        out_specs=pl.BlockSpec((step,) + shape, lambda i: (i, 0, 0)),
        out_shape=jax.ShapeDtypeStruct((experts,) + shape, pieces.dtype),
        cost_estimate=cost(4 * pieces.size, 0),
    )(pieces)


def exchange(pieces):
    return lax.all_to_all(pieces, "zero", split_axis=0, concat_axis=0, tiled=True)


def mine(scale, zero):
    width = scale.shape[1] // zero
    return lax.dynamic_slice_in_dim(scale, lax.axis_index("zero") * width, width, axis=1)


def aligned_device(sizes, mg, sg, mu, su, md, sd, router_weight, router_gain):
    bank, zero = sizes
    experts, rows, width = mg.shape
    model = rows * zero

    part_router = (router_weight * router_gain[:, None]).astype(bf16)
    router = to_all(part_router.reshape(-1, 128), ("bank", "zero"), bank * zero)

    part_up = jnp.sum(jnp.abs(mu + su.astype(f32)), axis=1)
    part_up, router = lax.optimization_barrier((part_up, router))
    all_up = to_all(part_up, "zero", zero)
    all_gate = to_all(jnp.sum(jnp.abs(mg + sg.astype(f32)), axis=1), "zero", zero)
    merged_down = md + sd.astype(f32)
    part_down = jnp.sum(jnp.abs(merged_down), axis=2)
    all_gate, all_up, part_down = lax.optimization_barrier((all_gate, all_up, part_down))
    all_down = to_all(part_down, "zero", zero)

    scale_gate = jnp.sum(all_gate, axis=0) / model
    narrow_gate = narrow_columns(mg, sg, (1.0 / scale_gate)[:, None, :], zero)
    narrow_gate, all_up, all_down = lax.optimization_barrier((narrow_gate, all_up, all_down))
    got_gate = exchange(narrow_gate)

    scale_up = jnp.sum(all_up, axis=0) / model
    narrow_up = narrow_columns(mu, su, (1.0 / scale_up)[:, None, :], zero)
    got_up = exchange(narrow_up)

    scale_down = jnp.sum(all_down, axis=0) / model
    narrow_down = (merged_down * (1.0 / scale_down)[:, :, None]).astype(bf16)
    split_down = narrow_down.reshape(experts, zero, width // zero, rows).transpose(1, 0, 2, 3)
    got_down = exchange(split_down)

    serve_router = (
        router.reshape(bank, zero, *part_router.shape).transpose(1, 2, 0, 3).reshape(model, -1)
    )
    return (
        join(got_gate, 1),
        join(got_up, 1),
        join(got_down, 2),
        mine(scale_gate, zero),
        mine(scale_up, zero),
        mine(scale_down, zero),
        serve_router,
    )


def general_device(sizes, mg, sg, mu, su, md, sd, router_weight, router_gain):
    zero = sizes[1]
    model = mg.shape[1] * zero
    merged = (mg + sg.astype(f32), mu + su.astype(f32), md + sd.astype(f32))
    totals = lax.psum(
        tuple(jnp.sum(jnp.abs(m), axis=a) for m, a in zip(merged, (1, 1, 2))), "zero"
    )
    scales = tuple(t / model for t in totals)
    finals = tuple(
        lax.all_to_all(
            (m / jnp.expand_dims(s, a)).astype(bf16),
            "zero", split_axis=3 - a, concat_axis=a, tiled=True,
        )
        for m, s, a in zip(merged, scales, (1, 1, 2))
    )
    part_router = (router_weight * router_gain[:, None]).astype(bf16)
    row_router = lax.all_gather(part_router, "zero", axis=0, tiled=True)
    serve_router = lax.all_gather(row_router, "bank", axis=1, tiled=True)
    return finals + tuple(mine(s, zero) for s in scales) + (serve_router,)


def solution(mesh):
    sizes = (mesh.shape["bank"], mesh.shape["zero"])

    def on_device(*args):
        _, rows, width = args[0].shape
        piece = width // sizes[1]
        tiles = piece % 128 == 0 and rows % 128 == 0 and args[6].size % 128 == 0
        return (aligned_device if tiles else general_device)(sizes, *args)

    return jax.shard_map(
        on_device,
        mesh=mesh,
        in_specs=(
            P("bank", "zero", None),
            P("bank", "zero", None),
            P("bank", "zero", None),
            P("bank", "zero", None),
            P("bank", None, "zero"),
            P("bank", None, "zero"),
            P("zero", "bank"),
            P("zero"),
        ),
        out_specs=(
            P("bank", None, "zero"),
            P("bank", None, "zero"),
            P("bank", "zero", None),
            P("bank", "zero"),
            P("bank", "zero"),
            P("bank", "zero"),
            P(),
        ),
        check_vma=False,
    )
```

time: 557 us -> 375 us (0.67)
  blocking collectives: 112 us -> 0 us
  local copies, waits for them, and re-layouts: 112 us -> 16.7 us
  Pallas kernels: 0 us -> 54.1 us
  other arithmetic: 87.4 us -> 40.3 us
  starting transfers between devices: 15.3 us -> 33.1 us
  waiting for transfers between devices: 214 us -> 228 us
  between operations: 14.1 us -> 0.77 us
    all_gather x2 -> x0, blocking collectives: 112 us -> none  [the longest x1 97.2 us: on_device(): row_router = lax.all_gather(part_router, 'zero', axis=0, tiled=True)]
    all_to_all x3 -> x7, waiting for transfers between devices: 152 us -> 228 us  [the longest x3 226 us: exchange(): lax.all_to_all(pieces, 'zero', split_axis=0, concat_axis=0, tiled=True)]
    unnamed x20 -> x1, local copies, waits for them, and re-layouts: 62.9 us -> 0.76 us
    psum x1 -> x0, waiting for transfers between devices: 62 us -> none  [on_device(): lax.psum((jnp.sum(jnp.abs(merged_gate), axis=1), jnp.sum(jnp.abs(merged_u...]
    pallas_call x0 -> x5, Pallas kernels: none -> 54.1 us  [the longest x3 27.1 us: join(): pl.pallas_call(body, grid=(experts // step,), in_specs=[pl.BlockSpec((zer...]
    all_to_all x4 -> x0, local copies, waits for them, and re-layouts: 49.4 us -> none  [the longest x2 24.8 us: on_device(): lax.all_to_all(narrow_down, 'zero', split_axis=1, concat_axis=2, tiled=True)]
    convert_element_type x4 -> x2, other arithmetic: 47.7 us -> 12.7 us  [the longest x1 12 us: aligned_device(): narrow_down = (merged_down * (1.0 / scale_down)[:, :, None]).astype(bf16)]
    all_to_all x3 -> x7, starting transfers between devices: 15.2 us -> 33.1 us  [the longest x4 18.1 us: to_all(): return lax.all_to_all(same, axes, split_axis=0, concat_axis=0, tiled=True)]
  transfers between devices with their start and end apart: 4 -> 7, of which waited for: 3 -> 6; matrix products, arithmetic and copies ran while one was open for 11% -> 14% of each run, Pallas kernels for 0% -> 12%
where the time goes in v1:
time: 375 us; the launch traced here: 373 us
  waiting for transfers between devices  228 us (61%)
  Pallas kernels  54.1 us (14%)
  other arithmetic  40.3 us (11%)
  starting transfers between devices  33.1 us (9%)
  local copies, waits for them, and re-layouts  16.7 us (4%)
    all_to_all x3, waiting for transfers between devices, exchange(): lax.all_to_all(pieces, 'zero', split_axis=0, concat_axis=0, tiled=True)  226 us
    pallas_call x3, Pallas kernels, join(): pl.pallas_call(body, grid=(experts // step,), in_specs=[pl.BlockSpec((zer...  27.1 us
    pallas_call x2, Pallas kernels, narrow_columns(): pl.pallas_call(body, grid=(experts // step,), in_specs=[block, block, pl....  27 us
    all_to_all x4, starting transfers between devices, to_all(): return lax.all_to_all(same, axes, split_axis=0, concat_axis=0, tiled=True)  18.1 us
    all_to_all x3, starting transfers between devices, exchange(): lax.all_to_all(pieces, 'zero', split_axis=0, concat_axis=0, tiled=True)  15 us
    convert_element_type x1, other arithmetic, aligned_device(): narrow_down = (merged_down * (1.0 / scale_down)[:, :, None]).astype(bf16)  12 us
    reduce_sum x1, other arithmetic, aligned_device(): jnp.sum(jnp.abs(mg + sg.astype(f32)), axis=1)  9.19 us
    reduce_sum x1, other arithmetic, aligned_device(): part_up = jnp.sum(jnp.abs(mu + su.astype(f32)), axis=1)  9.19 us
  transfers between devices with their start and end apart: 7, of which 6 were waited for; matrix products, arithmetic and copies ran while one was open for 14% of the time, Pallas kernels for 12%

profile of v1, /device:TPU:0, one launch (start us, length us, event | category | flops | bytes accessed | tf_op | source)
XLA Modules:
  0.0 373.5 jit_solution(12195049700325673007)
XLA Ops:
  2.3 7.3 %all-to-all-start.1 = ((bf16[32,32,128]{2,1,0:T(8,128)(2,1)}), bf16[32,32,128]{2,1,0:T(8,128)(2,1)S(1)}, u32[]{:S(2)}, u32[]{:S(2)}) async-start(bf16[32,32,128]{2,1,0:T(8,128)(2,1)} %broadcast_in_dim.12), calls=%async_computation.1 | async-start | bytes 524288 | tf_op jit(solution)/shard_map/all_to_all | solution.py:17
  9.7 9.2 %abs_reduce_fusion.2 = f32[16,1024]{1,0:T(8,128)S(1)} fusion(f32[16,256,1024]{2,1,0:T(8,128)} %master_ref.2, bf16[16,256,1024]{2,1,0:T(8,128)(2,1)} %second_ref.2), kind=kLoop, calls=%fused_computation.4 | loop fusion | flops 16760832 | bytes 25231360 | tf_op jit(solution)/shard_map/reduce_sum | solution.py:84
  18.9 1.4 all-to-all-done.1
  21.1 3.5 all-to-all-start
  24.6 9.2 %abs_reduce_fusion.1 = f32[16,1024]{1,0:T(8,128)S(1)} fusion(f32[16,256,1024]{2,1,0:T(8,128)} %master_ref.3, bf16[16,256,1024]{2,1,0:T(8,128)(2,1)} %second_ref.3), kind=kLoop, calls=%fused_computation.3 | loop fusion | flops 16760832 | bytes 25231360 | tf_op jit(solution)/shard_map/reduce_sum | solution.py:81
  34.2 0.8 broadcast_in_dim.13
  35.1 3.7 all-to-all-start.2
  38.8 9.1 %abs_reduce_fusion = f32[16,1024]{1,0:T(8,128)S(1)} fusion(f32[16,1024,256]{2,1,0:T(8,128)} %param.12, bf16[16,1024,256]{2,1,0:T(8,128)(2,1)} %param.13), kind=kLoop, calls=%fused_computation.1 | loop fusion | flops 16760832 | bytes 25231360 | tf_op jit(solution)/shard_map/reduce_sum | solution.py:86
  49.3 3.6 all-to-all-start.3
  53.7 13.5 %shard_map.135 = bf16[8,16,256,128]{3,2,1,0:T(8,128)(2,1)} custom-call(f32[16,256,1024]{2,1,0:T(8,128)} %master_ref.2, bf16[16,256,1024]{2,1,0:T(8,128)(2,1)} %second_ref.2, f32[16,1,1024]{2,1,0:T(1,128)} %copy.20.inverse_ref), custom_call_target="tpu_custom_call" | custom-call | flops 8388608 | bytes 33554432 | tf_op jit(solution)/shard_map/pallas_call | solution.py:32
  67.2 5.0 %all-to-all-start.4 = ((bf16[8,16,256,128]{3,2,1,0:T(8,128)(2,1)}), bf16[8,16,256,128]{3,2,1,0:T(8,128)(2,1)}, u32[]{:S(2)}, u32[]{:S(2)}) async-start(bf16[8,16,256,128]{3,2,1,0:T(8,128)(2,1)} %shard_map.135), calls=%async_computation.4 | async-start | bytes 16777216 | tf_op jit(solution)/shard_map/all_to_all | solution.py:65
  72.9 13.5 %shard_map.137 = bf16[8,16,256,128]{3,2,1,0:T(8,128)(2,1)} custom-call(f32[16,256,1024]{2,1,0:T(8,128)} %master_ref.3, bf16[16,256,1024]{2,1,0:T(8,128)(2,1)} %second_ref.3, f32[16,1,1024]{2,1,0:T(1,128)} %div.47.inverse_ref), custom_call_target="tpu_custom_call" | custom-call | flops 8388608 | bytes 33554432 | tf_op jit(solution)/shard_map/pallas_call | solution.py:32
  86.4 79.8 %all-to-all-done.4.in_ref = bf16[8,16,256,128]{3,2,1,0:T(8,128)(2,1)} async-done(((bf16[8,16,256,128]{3,2,1,0:T(8,128)(2,1)}), bf16[8,16,256,128]{3,2,1,0:T(8,128)(2,1)}, u32[]{:S(2)}, u32[]{:S(2)}) %all-to-all-start.4) | async-done | bytes 8388640 | tf_op jit(solution)/shard_map/all_to_all | solution.py:65
  166.2 5.0 %all-to-all-start.5 = ((bf16[8,16,256,128]{3,2,1,0:T(8,128)(2,1)}), bf16[8,16,256,128]{3,2,1,0:T(8,128)(2,1)}, u32[]{:S(2)}, u32[]{:S(2)}) async-start(bf16[8,16,256,128]{3,2,1,0:T(8,128)(2,1)} %shard_map.137), calls=%async_computation.5 | async-start | bytes 16777216 | tf_op jit(solution)/shard_map/all_to_all | solution.py:65
  171.3 12.0 %multiply_convert_fusion = bf16[16,1024,256]{2,1,0:T(8,128)(2,1)} fusion(f32[16,1024,256]{2,1,0:T(8,128)} %param.12, bf16[16,1024,256]{2,1,0:T(8,128)(2,1)} %param.13, f32[16,1024]{1,0:T(8,128)S(1)} %get-tuple-element.24), kind=kLoop, calls=%fused_computation | loop fusion | flops 16777216 | bytes 33619968 | tf_op jit(solution)/shard_map/convert_element_type | solution.py:100
  183.3 7.7 %copy.25 = bf16[16,8,128,256]{3,2,0,1:T(8,128)(2,1)} copy(bf16[16,8,128,256]{3,2,1,0:T(8,128)(2,1)} %bitcast.13) | data formatting | bytes 16777216 | tf_op jit(solution)/shard_map/reshape | solution.py:101
  191.0 74.3 %all-to-all-done.5.in_ref = bf16[8,16,256,128]{3,2,1,0:T(8,128)(2,1)} async-done(((bf16[8,16,256,128]{3,2,1,0:T(8,128)(2,1)}), bf16[8,16,256,128]{3,2,1,0:T(8,128)(2,1)}, u32[]{:S(2)}, u32[]{:S(2)}) %all-to-all-start.5) | async-done | bytes 8388640 | tf_op jit(solution)/shard_map/all_to_all | solution.py:65
  265.3 5.0 %all-to-all-start.6 = ((bf16[8,16,128,256]{3,2,1,0:T(8,128)(2,1)}), bf16[8,16,128,256]{3,2,1,0:T(8,128)(2,1)}, u32[]{:S(2)}, u32[]{:S(2)}) async-start(bf16[8,16,128,256]{3,2,1,0:T(8,128)(2,1)} %bitcast.12), calls=%async_computation.6 | async-start | bytes 16777216 | tf_op jit(solution)/shard_map/all_to_all | solution.py:65
  270.3 1.4 reshape.61
  271.6 0.9 copy.22
  274.5 9.0 %shard_map.136 = bf16[16,2048,128]{2,1,0:T(8,128)(2,1)} custom-call(bf16[8,16,256,128]{3,2,1,0:T(8,128)(2,1)} %all-to-all-done.4.in_ref), custom_call_target="tpu_custom_call" | custom-call | bytes 16777216 | tf_op jit(solution)/shard_map/pallas_call | solution.py:54
  283.4 9.0 %shard_map.138 = bf16[16,2048,128]{2,1,0:T(8,128)(2,1)} custom-call(bf16[8,16,256,128]{3,2,1,0:T(8,128)(2,1)} %all-to-all-done.5.in_ref), custom_call_target="tpu_custom_call" | custom-call | bytes 16777216 | tf_op jit(solution)/shard_map/pallas_call | solution.py:54
  292.4 71.9 %all-to-all-done.6.in_ref = bf16[8,16,128,256]{3,2,1,0:T(8,128)(2,1)} async-done(((bf16[8,16,128,256]{3,2,1,0:T(8,128)(2,1)}), bf16[8,16,128,256]{3,2,1,0:T(8,128)(2,1)}, u32[]{:S(2)}, u32[]{:S(2)}) %all-to-all-start.6) | async-done | bytes 8388640 | tf_op jit(solution)/shard_map/all_to_all | solution.py:65
  364.3 9.2 %shard_map.139 = bf16[16,128,2048]{2,1,0:T(8,128)(2,1)} custom-call(bf16[8,16,128,256]{3,2,1,0:T(8,128)(2,1)} %all-to-all-done.6.in_ref), custom_call_target="tpu_custom_call" | custom-call | bytes 16777216 | tf_op jit(solution)/shard_map/pallas_call | solution.py:54
  (20 shorter events, 7.9 us)
Async XLA Ops:
  2.3 17.9 %all-to-all-start.1 = ((bf16[32,32,128]{2,1,0:T(8,128)(2,1)}), bf16[32,32,128]{2,1,0:T(8,128)(2,1)S(1)}, u32[]{:S(2)}, u32[]{:S(2)}) async-start(bf16[32,32,128]{2,1,0:T(8,128)(2,1)} %broadcast_in_dim.12), calls=%async_computation.1 | async-start | bytes 524288 | tf_op jit(solution)/shard_map/all_to_all | solution.py:17
  21.1 13.2 %all-to-all-start = ((f32[8,16,1024]{2,1,0:T(8,128)}), f32[8,16,1024]{2,1,0:T(8,128)S(1)}, u32[]{:S(2)}, u32[]{:S(2)}) async-start(f32[8,16,1024]{2,1,0:T(8,128)} %broadcast_in_dim.10), calls=%async_computation | async-start | bytes 1048576 | tf_op jit(solution)/shard_map/all_to_all | solution.py:17
  35.1 13.4 %all-to-all-start.2 = ((f32[8,16,1024]{2,1,0:T(8,128)}), f32[8,16,1024]{2,1,0:T(8,128)S(1)}, u32[]{:S(2)}, u32[]{:S(2)}) async-start(f32[8,16,1024]{2,1,0:T(8,128)} %broadcast_in_dim.13), calls=%async_computation.2 | async-start | bytes 1048576 | tf_op jit(solution)/shard_map/all_to_all | solution.py:17
  49.3 17.9 %all-to-all-start.3 = ((f32[8,16,1024]{2,1,0:T(8,128)}), f32[8,16,1024]{2,1,0:T(8,128)S(1)}, u32[]{:S(2)}, u32[]{:S(2)}) async-start(f32[8,16,1024]{2,1,0:T(8,128)} %broadcast_in_dim.14), calls=%async_computation.3 | async-start | bytes 1048576 | tf_op jit(solution)/shard_map/all_to_all | solution.py:17
  67.2 99.0 %all-to-all-start.4 = ((bf16[8,16,256,128]{3,2,1,0:T(8,128)(2,1)}), bf16[8,16,256,128]{3,2,1,0:T(8,128)(2,1)}, u32[]{:S(2)}, u32[]{:S(2)}) async-start(bf16[8,16,256,128]{3,2,1,0:T(8,128)(2,1)} %shard_map.135), calls=%async_computation.4 | async-start | bytes 16777216 | tf_op jit(solution)/shard_map/all_to_all | solution.py:65
  166.2 99.1 %all-to-all-start.5 = ((bf16[8,16,256,128]{3,2,1,0:T(8,128)(2,1)}), bf16[8,16,256,128]{3,2,1,0:T(8,128)(2,1)}, u32[]{:S(2)}, u32[]{:S(2)}) async-start(bf16[8,16,256,128]{3,2,1,0:T(8,128)(2,1)} %shard_map.137), calls=%async_computation.5 | async-start | bytes 16777216 | tf_op jit(solution)/shard_map/all_to_all | solution.py:65
  265.3 99.0 %all-to-all-start.6 = ((bf16[8,16,128,256]{3,2,1,0:T(8,128)(2,1)}), bf16[8,16,128,256]{3,2,1,0:T(8,128)(2,1)}, u32[]{:S(2)}, u32[]{:S(2)}) async-start(bf16[8,16,128,256]{3,2,1,0:T(8,128)(2,1)} %bitcast.12), calls=%async_computation.6 | async-start | bytes 16777216 | tf_op jit(solution)/shard_map/all_to_all | solution.py:65
